TPU v7x, 32 devices: a whole 2x2x4 slice. The times are simulated.
32 devices in a mesh: fsdp: 16 (over z, y, core), dp: 2 (over x).
Axes of the slice: x: 2, y: 2, z: 4, core: 2. Of those that a mesh axis runs over, the one named last changes fastest.
Arguments:
- block_input: bfloat16 [160, 416, 768], P(('fsdp', 'dp')), may hold values from -6 to 6
- segment_ids: int32 [160, 416], P(('fsdp', 'dp')), may hold values from -1 to 24, as said below
- ln1_gain: bfloat16 [768], P('fsdp'), may hold values from 0.099609375 to 1.8984375
- ln1_bias: bfloat16 [768], P('fsdp'), may hold values from -3 to 3
- qkv_weight: bfloat16 [768, 2304], P('fsdp'), may hold values from -0.21875 to 0.21875
- qv_bias: bfloat16 [1536], P('fsdp'), may hold values from -3 to 3
- out_weight: bfloat16 [768, 768], P('fsdp'), may hold values from -0.875 to 0.875
- out_bias: bfloat16 [768], P('fsdp'), may hold values from -3 to 3
- ln2_gain: bfloat16 [768], P('fsdp'), may hold values from 0.099609375 to 1.8984375
- ln2_bias: bfloat16 [768], P('fsdp'), may hold values from -3 to 3
- up_weight: bfloat16 [768, 3072], P('fsdp'), may hold values from -0.21875 to 0.21875
- up_bias: bfloat16 [3072], P('fsdp'), may hold values from -3 to 3
- down_weight: bfloat16 [3072, 768], P('fsdp'), may hold values from -0.109375 to 0.109375
- down_bias: bfloat16 [768], P('fsdp'), may hold values from -3 to 3
- out_cotangent: bfloat16 [160, 416, 768], P(('fsdp', 'dp')), may hold values from -6 to 6
Outputs:
- block_output: bfloat16 [160, 416, 768], P(('fsdp', 'dp'))
- input_grad: bfloat16 [160, 416, 768], P(('fsdp', 'dp'))
- ln1_gain_grad: float32 [768], P('fsdp')
- ln1_bias_grad: float32 [768], P('fsdp')
- qkv_weight_grad: float32 [768, 2304], P('fsdp')
- qv_bias_grad: float32 [1536], P('fsdp')
- out_weight_grad: float32 [768, 768], P('fsdp')
- out_bias_grad: float32 [768], P('fsdp')
- ln2_gain_grad: float32 [768], P('fsdp')
- ln2_bias_grad: float32 [768], P('fsdp')
- up_weight_grad: float32 [768, 3072], P('fsdp')
- up_bias_grad: float32 [3072], P('fsdp')
- down_weight_grad: float32 [3072, 768], P('fsdp')
- down_bias_grad: float32 [768], P('fsdp')
Inputs may be any that keep to these rules, and one draw needn't show every extreme that they name: `segment_ids`: each packed row holds whole images of h x w slots with h and w from 4 to 14, numbered 0, 1, 2 in order from the row's start, followed by padding slots marked -1 (at least one in every row); some row holds the most images that fit.
All inputs are finite; a program needn't handle non-finite values.
Results may differ from a plain program's by a relative error of at most 0.013.
Values may be sent and summed in bfloat16 or wider, within the bound.
A program may use at most 256 MiB of HBM per device.

v0:
```python
import jax
import jax.numpy as jnp
from jax import lax
from jax.sharding import PartitionSpec as P

HEAD_DIM = 64


def layer_norm(values, gain, shift):
    center = values - jnp.mean(values, axis=-1, keepdims=True)
    spread = jnp.mean(center * center, axis=-1, keepdims=True)
    return center * lax.rsqrt(spread + 1e-06) * gain + shift


def gelu_exact(values):
    return jax.nn.gelu(values, approximate=False)


def masked_scores(queries, keys_row, segment_row):
    scores = (
        jnp.einsum("qhe,khe->hqk", queries, keys_row, preferred_element_type=jnp.float32) * 0.125
    )
    allowed = segment_row[:, None] == segment_row[None, :]
    return jnp.where(allowed[None], scores, -jnp.inf)


def row_forward(items):
    queries, keys_row, values_row, segment_row = items
    scores = masked_scores(queries, keys_row, segment_row)
    highest = jnp.max(scores, axis=-1, keepdims=True)
    expo = jnp.exp(scores - highest)
    totals = jnp.sum(expo, axis=-1, keepdims=True)
    probs = (expo / totals).astype(jnp.bfloat16)
    mixed = jnp.einsum("hqk,khe->qhe", probs, values_row, preferred_element_type=jnp.float32)
    return (mixed.astype(jnp.bfloat16), (highest + jnp.log(totals))[..., 0])


def row_backward(items):
    queries, keys_row, values_row, segment_row, grad_mixed, logsum = items
    scores = masked_scores(queries, keys_row, segment_row)
    probs = jnp.exp(scores - logsum[..., None])
    grad_probs = jnp.einsum(
        "qhe,khe->hqk", grad_mixed, values_row, preferred_element_type=jnp.float32
    )
    grad_values = jnp.einsum(
        "hqk,qhe->khe", probs.astype(jnp.bfloat16), grad_mixed, preferred_element_type=jnp.float32
    ).astype(jnp.bfloat16)
    inner = jnp.sum(probs * grad_probs, axis=-1, keepdims=True)
    grad_scores = (probs * (grad_probs - inner)).astype(jnp.bfloat16)
    grad_queries = (
        jnp.einsum("hqk,khe->qhe", grad_scores, keys_row, preferred_element_type=jnp.float32)
        * 0.125
    ).astype(jnp.bfloat16)
    grad_keys = (
        jnp.einsum("hqk,qhe->khe", grad_scores, queries, preferred_element_type=jnp.float32) * 0.125
    ).astype(jnp.bfloat16)
    return (grad_queries, grad_keys, grad_values)


def per_device(
    block_input,
    segment_ids,
    ln1_gain,
    ln1_bias,
    qkv_weight,
    qv_bias,
    out_weight,
    out_bias,
    ln2_gain,
    ln2_bias,
    up_weight,
    up_bias,
    down_weight,
    down_bias,
    out_cotangent,
):
    rows, slots, width = block_input.shape
    heads = width // HEAD_DIM
    shape_four = (rows, slots, heads, HEAD_DIM)
    attn_shards = (ln1_gain, ln1_bias, qkv_weight, qv_bias, out_weight, out_bias)
    mlp_shards = (ln2_gain, ln2_bias, up_weight, up_bias, down_weight, down_bias)
    attn_full = (
        lax.all_gather(attn_shards[0], "fsdp", axis=0, tiled=True),
        lax.all_gather(attn_shards[1], "fsdp", axis=0, tiled=True),
        lax.all_gather(attn_shards[2], "fsdp", axis=0, tiled=True),
        lax.all_gather(attn_shards[3], "fsdp", axis=0, tiled=True),
        lax.all_gather(attn_shards[4], "fsdp", axis=0, tiled=True),
        lax.all_gather(attn_shards[5], "fsdp", axis=0, tiled=True),
    )
    gain_one, shift_one, qkv_full, bias_full, proj_full, proj_bias = attn_full
    flat = block_input.reshape(-1, width).astype(jnp.float32)
    normed, norm_back = jax.vjp(
        layer_norm, flat, gain_one.astype(jnp.float32), shift_one.astype(jnp.float32)
    )
    normed_low = normed.astype(jnp.bfloat16)
    projected = jnp.dot(normed_low, qkv_full, preferred_element_type=jnp.float32)
    bias_wide = bias_full.astype(jnp.float32)
    queries = (projected[:, :width] + bias_wide[:width]).astype(jnp.bfloat16).reshape(shape_four)
    keys_all = projected[:, width : 2 * width].astype(jnp.bfloat16).reshape(shape_four)
    values_all = (
        (projected[:, 2 * width :] + bias_wide[width:]).astype(jnp.bfloat16).reshape(shape_four)
    )
    mixed, logsum = lax.map(row_forward, (queries, keys_all, values_all, segment_ids))
    mixed_flat = mixed.reshape(-1, width)
    middle = (
        flat
        + jnp.dot(mixed_flat, proj_full, preferred_element_type=jnp.float32)
        + proj_bias.astype(jnp.float32)
    )
    mlp_full = (
        lax.all_gather(mlp_shards[0], "fsdp", axis=0, tiled=True),
        lax.all_gather(mlp_shards[1], "fsdp", axis=0, tiled=True),
        lax.all_gather(mlp_shards[2], "fsdp", axis=0, tiled=True),
        lax.all_gather(mlp_shards[3], "fsdp", axis=0, tiled=True),
        lax.all_gather(mlp_shards[4], "fsdp", axis=0, tiled=True),
        lax.all_gather(mlp_shards[5], "fsdp", axis=0, tiled=True),
    )
    gain_two, shift_two, up_full, up_shift, down_full, down_shift = mlp_full
    normed_two, norm_two_back = jax.vjp(
        layer_norm, middle, gain_two.astype(jnp.float32), shift_two.astype(jnp.float32)
    )
    normed_two_low = normed_two.astype(jnp.bfloat16)
    hidden_pre = jnp.dot(
        normed_two_low, up_full, preferred_element_type=jnp.float32
    ) + up_shift.astype(jnp.float32)
    hidden_act, gelu_back = jax.vjp(gelu_exact, hidden_pre)
    hidden_low = hidden_act.astype(jnp.bfloat16)
    output = (
        middle
        + jnp.dot(hidden_low, down_full, preferred_element_type=jnp.float32)
        + down_shift.astype(jnp.float32)
    )
    block_output = output.astype(jnp.bfloat16).reshape(rows, slots, width)
    mlp_again = (
        lax.all_gather(mlp_shards[0], "fsdp", axis=0, tiled=True),
        lax.all_gather(mlp_shards[1], "fsdp", axis=0, tiled=True),
        lax.all_gather(mlp_shards[2], "fsdp", axis=0, tiled=True),
        lax.all_gather(mlp_shards[3], "fsdp", axis=0, tiled=True),
        lax.all_gather(mlp_shards[4], "fsdp", axis=0, tiled=True),
        lax.all_gather(mlp_shards[5], "fsdp", axis=0, tiled=True),
    )
    up_back = mlp_again[2]
    down_back = mlp_again[4]
    cotangent = out_cotangent.reshape(-1, width)
    cot_wide = cotangent.astype(jnp.float32)
    down_bias_grad = jnp.sum(cot_wide, axis=0)
    down_weight_grad = jnp.einsum(
        "nf,nd->fd", hidden_low, cotangent, preferred_element_type=jnp.float32
    )
    grad_hidden = jnp.einsum("nd,fd->nf", cotangent, down_back, preferred_element_type=jnp.float32)
    grad_pre = gelu_back(grad_hidden)[0].astype(jnp.bfloat16)
    up_bias_grad = jnp.sum(grad_pre.astype(jnp.float32), axis=0)
    up_weight_grad = jnp.einsum(
        "nd,nf->df", normed_two_low, grad_pre, preferred_element_type=jnp.float32
    )
    grad_normed_two = jnp.einsum("nf,df->nd", grad_pre, up_back, preferred_element_type=jnp.float32)
    grad_mid_norm, gain_two_grad, shift_two_grad = norm_two_back(grad_normed_two)
    grad_middle = cot_wide + grad_mid_norm
    mlp_local = (
        gain_two_grad,
        shift_two_grad,
        up_weight_grad,
        up_bias_grad,
        down_weight_grad,
        down_bias_grad,
    )
    mlp_owned = (
        lax.psum_scatter(mlp_local[0], "fsdp", scatter_dimension=0, tiled=True),
        lax.psum_scatter(mlp_local[1], "fsdp", scatter_dimension=0, tiled=True),
        lax.psum_scatter(mlp_local[2], "fsdp", scatter_dimension=0, tiled=True),
        lax.psum_scatter(mlp_local[3], "fsdp", scatter_dimension=0, tiled=True),
        lax.psum_scatter(mlp_local[4], "fsdp", scatter_dimension=0, tiled=True),
        lax.psum_scatter(mlp_local[5], "fsdp", scatter_dimension=0, tiled=True),
    )
    mlp_summed = (
        lax.psum(mlp_owned[0].astype(jnp.bfloat16), "dp").astype(jnp.float32),
        lax.psum(mlp_owned[1].astype(jnp.bfloat16), "dp").astype(jnp.float32),
        lax.psum(mlp_owned[2].astype(jnp.bfloat16), "dp").astype(jnp.float32),
        lax.psum(mlp_owned[3].astype(jnp.bfloat16), "dp").astype(jnp.float32),
        lax.psum(mlp_owned[4].astype(jnp.bfloat16), "dp").astype(jnp.float32),
        lax.psum(mlp_owned[5].astype(jnp.bfloat16), "dp").astype(jnp.float32),
    )
    attn_again = (
        lax.all_gather(attn_shards[0], "fsdp", axis=0, tiled=True),
        lax.all_gather(attn_shards[1], "fsdp", axis=0, tiled=True),
        lax.all_gather(attn_shards[2], "fsdp", axis=0, tiled=True),
        lax.all_gather(attn_shards[3], "fsdp", axis=0, tiled=True),
        lax.all_gather(attn_shards[4], "fsdp", axis=0, tiled=True),
        lax.all_gather(attn_shards[5], "fsdp", axis=0, tiled=True),
    )
    qkv_back = attn_again[2]
    proj_back = attn_again[4]
    grad_branch = grad_middle.astype(jnp.bfloat16)
    out_bias_grad = jnp.sum(grad_branch.astype(jnp.float32), axis=0)
    out_weight_grad = jnp.einsum(
        "nd,ne->de", mixed_flat, grad_branch, preferred_element_type=jnp.float32
    )
    grad_mixed = jnp.einsum(
        "ne,de->nd", grad_branch, proj_back, preferred_element_type=jnp.float32
    ).astype(jnp.bfloat16)
    grad_queries, grad_keys, grad_values = lax.map(
        row_backward,
        (queries, keys_all, values_all, segment_ids, grad_mixed.reshape(shape_four), logsum),
    )
    grad_queries = grad_queries.reshape(-1, width)
    grad_keys = grad_keys.reshape(-1, width)
    grad_values = grad_values.reshape(-1, width)
    grad_projected = jnp.concatenate([grad_queries, grad_keys, grad_values], axis=1)
    qv_bias_grad = jnp.concatenate(
        [
            jnp.sum(grad_queries.astype(jnp.float32), axis=0),
            jnp.sum(grad_values.astype(jnp.float32), axis=0),
        ]
    )
    qkv_weight_grad = jnp.einsum(
        "nd,nc->dc", normed_low, grad_projected, preferred_element_type=jnp.float32
    )
    grad_normed = jnp.einsum(
        "nc,dc->nd", grad_projected, qkv_back, preferred_element_type=jnp.float32
    )
    grad_flat_norm, gain_one_grad, shift_one_grad = norm_back(grad_normed)
    input_grad = (grad_middle + grad_flat_norm).astype(jnp.bfloat16).reshape(rows, slots, width)
    attn_local = (
        gain_one_grad,
        shift_one_grad,
        qkv_weight_grad,
        qv_bias_grad,
        out_weight_grad,
        out_bias_grad,
    )
    attn_owned = (
        lax.psum_scatter(attn_local[0], "fsdp", scatter_dimension=0, tiled=True),
        lax.psum_scatter(attn_local[1], "fsdp", scatter_dimension=0, tiled=True),
        lax.psum_scatter(attn_local[2], "fsdp", scatter_dimension=0, tiled=True),
        lax.psum_scatter(attn_local[3], "fsdp", scatter_dimension=0, tiled=True),
        lax.psum_scatter(attn_local[4], "fsdp", scatter_dimension=0, tiled=True),
        lax.psum_scatter(attn_local[5], "fsdp", scatter_dimension=0, tiled=True),
    )
    attn_summed = (
        lax.psum(attn_owned[0].astype(jnp.bfloat16), "dp").astype(jnp.float32),
        lax.psum(attn_owned[1].astype(jnp.bfloat16), "dp").astype(jnp.float32),
        lax.psum(attn_owned[2].astype(jnp.bfloat16), "dp").astype(jnp.float32),
        lax.psum(attn_owned[3].astype(jnp.bfloat16), "dp").astype(jnp.float32),
        lax.psum(attn_owned[4].astype(jnp.bfloat16), "dp").astype(jnp.float32),
        lax.psum(attn_owned[5].astype(jnp.bfloat16), "dp").astype(jnp.float32),
    )
    return (
        block_output,
        input_grad,
        attn_summed[0],
        attn_summed[1],
        attn_summed[2],
        attn_summed[3],
        attn_summed[4],
        attn_summed[5],
        mlp_summed[0],
        mlp_summed[1],
        mlp_summed[2],
        mlp_summed[3],
        mlp_summed[4],
        mlp_summed[5],
    )


def solution(mesh):
    return jax.shard_map(
        per_device,
        mesh=mesh,
        in_specs=(
            P(("fsdp", "dp"), None, None),
            P(("fsdp", "dp"), None),
            P("fsdp"),
            P("fsdp"),
            P("fsdp", None),
            P("fsdp"),
            P("fsdp", None),
            P("fsdp"),
            P("fsdp"),
            P("fsdp"),
            P("fsdp", None),
            P("fsdp"),
            P("fsdp", None),
            P("fsdp"),
            P(("fsdp", "dp"), None, None),
        ),
        out_specs=(
            P(("fsdp", "dp"), None, None),
            P(("fsdp", "dp"), None, None),
            P("fsdp"),
            P("fsdp"),
            P("fsdp", None),
            P("fsdp"),
            P("fsdp", None),
            P("fsdp"),
            P("fsdp"),
            P("fsdp"),
            P("fsdp", None),
            P("fsdp"),
            P("fsdp", None),
            P("fsdp"),
        ),
        check_vma=False,
    )
```

profile of v0, /device:TPU:0, one launch (start us, length us, event | category | flops | bytes accessed | tf_op | source)
XLA Modules:
  0.0 992.4 jit_solution(8717277212317786385)
XLA Ops:
  20.1 64.0 %all-reduce.17 = (bf16[768]{0:T(1024)(128)(2,1)S(1)}, bf16[768]{0:T(1024)(128)(2,1)S(1)}, bf16[1536]{0:T(1024)(128)(2,1)S(1)}, bf16[768]{0:T(1024)(128)(2,1)S(1)...) all-reduce(bf16[768]{0:T(1024)(128)(2,1)S(1)} %dynamic-update-slice, ...), channel_id=1, replica_groups=mesh['fsdp'=16,'dp'=2] {'fsdp'}, use_global_device_ids=true, to_apply=%add.1 | all-reduce | flops 9216 | bytes 36864
  91.7 10.9 %fusion.78 = f32[2080,2304]{1,0:T(8,128)S(1)} fusion(bf16[2080,768]{1,0:T(8,128)(2,1)} %get-tuple-element.243, bf16[768,2304]{1,0:T(8,128)(2,1)} %all-gather.5.cloned.1.call-done), kind=kOutput, calls=%fused_computation.139 | convolution fusion | flops 7361003520 | bytes 25903104 | tf_op jit(solution)/shard_map/dot_general | solution.py:96
  107.0 10.8 %reshape.303 = bf16[5,416,12,64]{3,2,1,0:T(8,128)(2,1)} reshape(bf16[2080,768]{1,0:T(8,128)(2,1)} %get-tuple-element.241) | data formatting | bytes 6389760 | tf_op jit(solution)/shard_map/reshape | solution.py:101
  117.8 10.7 %copy.66 = bf16[5,416,12,64]{1,3,2,0:T(8,128)(2,1)} copy(bf16[5,416,12,64]{3,2,1,0:T(8,128)(2,1)} %reshape.303) | data formatting | bytes 6389760 | tf_op jit(solution)/shard_map/while | solution.py:103
  128.4 7.7 reshape.304
  136.1 10.8 %copy.67 = bf16[5,416,12,64]{1,3,2,0:T(8,128)(2,1)} copy(bf16[5,416,12,64]{3,2,1,0:T(8,128)(2,1)} %reshape.304) | data formatting | bytes 6389760 | tf_op jit(solution)/shard_map/while | solution.py:103
  147.0 8.1 reshape.305
  155.1 10.7 %copy.68 = bf16[5,416,12,64]{1,3,2,0:T(8,128)(2,1)} copy(bf16[5,416,12,64]{3,2,1,0:T(8,128)(2,1)} %reshape.305) | data formatting | bytes 6389760 | tf_op jit(solution)/shard_map/while | solution.py:103
  168.1 59.9 %while.26 = (s32[]{:T(128)}, bf16[5,416,12,64]{1,3,2,0:T(8,128)(2,1)}, f32[5,12,416]{2,1,0:T(8,128)}, bf16[5,416,12,64]{1,3,2,0:T(8,128)(2,1)}, s32[5,416]{1,0:T...) while((s32[]{:T(128)}, bf16[5,416,12,64]{1,3,2,0:T(8,128)(2,1)}, ...), condition=%wide.region_5.6_spmd, body=%wide.region_2.5_spmd.sunk | while | flops 557035648 | bytes 28938200 | solution.py:103
  228.0 7.7 copy.69
  235.7 9.7 reshape.245
  260.6 71.5 %multiply_convert_fusion.3 = (bf16[2080,3072]{1,0:T(8,128)(2,1)}, f32[2080,3072]{1,0:T(8,128)}, f32[2080,3072]{1,0:T(8,128)}) fusion(f32[3072]{0:T(1024)S(1)} %copy-done.33, bf16[768,3072]{1,0:T(8,128)(2,1)} %all-gather.9.cloned.1.call-done, f32[2080,768]{1,0:T(8,128)} %fusion.67, f32[768]{0:T(1024)S(1)} %copy-done.35, f32[768]{0:T(1024)S(1)} %copy-done.30, ...), kind=kOutput, calls=%fused_computation.68 | convolution fusion | flops 10244382720 | bytes 75041024 | tf_op jit(solution)/shard_map/dot_general | solution.py:123
  332.1 28.3 %convert_reduce_fusion = (f32[3072]{0:T(1024)}, bf16[2080,3072]{1,0:T(8,128)(2,1)}) fusion(f32[2080,3072]{1,0:T(8,128)} %get-tuple-element.235, bf16[2080,768]{1,0:T(8,128)(2,1)S(1)} %bitcast.159, bf16[3072,768]{1,0:T(8,128)(2,1)} %all-gather.11.cloned.1.call-done, f32[2080,3072]{1,0:T(8,128)} %get-tuple-element.248, f32[3072]{0:T(1024)S(1)} %copy-done.33), kind=kOutput, calls=%fused_computation.66 | convolution fusion | flops 9923294208 | bytes 71835648 | tf_op jit(solution)/shard_map/nd,fd->nf/dot_general | solution.py:150
  360.5 22.1 %multiply_reduce_fusion.1 = (f32[768]{0:T(1024)}, f32[2080]{0:T(1024)S(1)}, f32[768]{0:T(1024)}, f32[2080,768]{1,0:T(8,128)}) fusion(f32[2080,768]{1,0:T(8,128)} %fusion.67, f32[2080]{0:T(1024)S(1)} %fusion.69, f32[2080]{0:T(1024)S(1)} %broadcast_multiply_fusion.1, f32[768]{0:T(1024)S(1)} %copy-done.30, bf16[2080,3072]{1,0:T(8,128)(2,1)} %get-tuple-element.252, ...), kind=kOutput, calls=%fused_computation.98 | convolution fusion | flops 9827446784 | bytes 30311808 | tf_op jit(solution)/shard_map/nf,df->nd/dot_general | solution.py:156
  402.7 10.8 %reshape.294 = bf16[5,416,12,64]{3,2,1,0:T(8,128)(2,1)} reshape(bf16[2080,768]{1,0:T(8,128)(2,1)} %convolution_convert_fusion) | data formatting | bytes 6389760 | tf_op jit(solution)/shard_map/reshape | solution.py:203
  413.5 10.7 %copy.73 = bf16[5,416,12,64]{1,3,2,0:T(8,128)(2,1)} copy(bf16[5,416,12,64]{3,2,1,0:T(8,128)(2,1)} %reshape.294) | data formatting | bytes 6389760 | tf_op jit(solution)/shard_map/while | solution.py:201
  431.4 121.2 %while.27 = (s32[]{:T(128)}, bf16[5,416,12,64]{1,3,2,0:T(8,128)(2,1)}, bf16[5,416,12,64]{1,3,2,0:T(8,128)(2,1)}, bf16[5,416,12,64]{1,3,2,0:T(8,128)(2,1)}, bf16[...) while((s32[]{:T(128)}, ...), condition=%wide.region_12.13_spmd, body=%wide.region_10.12_spmd.sunk | while | flops 1361985664 | bytes 71006704 | solution.py:201
  552.6 7.7 copy.75
  560.4 8.4 reshape.249
  568.8 7.7 copy.76
  576.5 9.5 reshape.250
  586.0 7.7 copy.77
  593.8 9.5 reshape.251
  610.5 11.0 %fusion.79 = f32[768,2304]{1,0:T(8,128)} fusion(bf16[2080,768]{1,0:T(8,128)(2,1)S(1)} %copy-done.12, bf16[2080,2304]{0,1:T(8,128)(2,1)S(1)} %constant_dynamic-update-slice_fusion), kind=kOutput, calls=%fused_computation.140 | convolution fusion | flops 7361003520 | bytes 19857408 | tf_op jit(solution)/shard_map/nd,nc->dc/dot_general | solution.py:215
  622.3 19.4 %fusion.70 = f32[768,3072]{1,0:T(8,128)} fusion(bf16[2080,3072]{1,0:T(8,128)(2,1)} %get-tuple-element.252, f32[2080,768]{1,0:T(8,128)} %fusion.67, f32[768]{0:T(1024)S(1)} %copy-done.36, f32[768]{0:T(1024)S(1)} %copy-done.31, f32[2080]{0:T(1024)S(1)} %copy-done.27, f32[2080]{0:T(1024)S(1)} %copy-done.21), kind=kOutput, calls=%fused_computation.133 | convolution fusion | flops 9822658560 | bytes 28629248 | tf_op jit(solution)/shard_map/nd,nf->df/dot_general | solution.py:153
  643.6 15.7 %fusion.81 = f32[3072,768]{1,0:T(8,128)} fusion(bf16[2080,3072]{1,0:T(8,128)(2,1)} %get-tuple-element.234, bf16[2080,768]{1,0:T(8,128)(2,1)S(1)} %bitcast.160), kind=kOutput, calls=%fused_computation.142 | convolution fusion | flops 9814671360 | bytes 25411584 | tf_op jit(solution)/shard_map/nf,nd->fd/dot_general | solution.py:147
  668.9 19.5 %fusion.72 = (f32[768]{0:T(1024)S(1)}, f32[2080]{0:T(1024)S(1)}, f32[768]{0:T(1024)S(1)}, f32[2080,768]{1,0:T(8,128)}) fusion(f32[2080,768]{1,0:T(8,128)} %get-tuple-element.242, f32[768]{0:T(1024)S(1)} %copy-done.29, f32[2080]{0:T(1024)S(1)} %copy-done.17, f32[2080]{0:T(1024)S(1)} %copy-done.15, bf16[5,416,768]{2,1,0:T(8,128)(2,1)S(1)} %copy-done.4, ...), kind=kOutput, calls=%fused_computation.135 | convolution fusion | flops 7375376384 | bytes 29132160 | tf_op jit(solution)/shard_map/nc,dc->nd/dot_general | solution.py:218
  688.7 58.4 %all-reduce.16 = (bf16[768]{0:T(1024)(128)(2,1)S(1)}, bf16[768]{0:T(1024)(128)(2,1)S(1)}, bf16[1536]{0:T(1024)(128)(2,1)S(1)}, bf16[768]{0:T(1024)(128)(2,1)S(1)...) all-reduce(f32[768]{0:T(1024)S(1)} %get-tuple-element.167, ...), channel_id=2, replica_groups=mesh['fsdp'=16,'dp'=2] {'fsdp'}, use_global_device_ids=true, to_apply=%region_16.17.clone | all-reduce | flops 9216 | bytes 55296
  767.2 16.9 %add_convert_fusion.2 = bf16[2080,768]{1,0:T(8,128)(2,1)} fusion(f32[2080,768]{1,0:T(8,128)} %fusion.67, bf16[2080,3072]{1,0:T(8,128)(2,1)} %get-tuple-element.234, bf16[3072,768]{1,0:T(8,128)(2,1)} %all-gather.11.cloned.1.call-done, f32[768]{0:T(1024)S(1)} %convert_element_type.205), kind=kOutput, calls=%fused_computation.105 | convolution fusion | flops 9819463680 | bytes 27085824 | tf_op jit(solution)/shard_map/dot_general | solution.py:130
  787.4 36.4 %reduce-scatter.9.cloned.1.call-done = f32[48,3072]{1,0:T(8,128)} async-done(((f32[768,3072]{1,0:T(8,128)}), f32[48,3072]{1,0:T(8,128)}) %reduce-scatter.9.cloned.1.call-update) | async-done | bytes 589840 | tf_op jit(solution)/shard_map/reduce_scatter | solution.py:170
  825.6 113.2 %reduce-scatter.11.cloned.1.call-done = f32[192,768]{1,0:T(8,128)} async-done(((f32[3072,768]{1,0:T(8,128)}), f32[192,768]{1,0:T(8,128)}) %reduce-scatter.11.cloned.1.call-update) | async-done | bytes 589840 | tf_op jit(solution)/shard_map/reduce_scatter | solution.py:172
  947.6 31.1 %all-reduce.22.cloned.1.call-done = (bf16[48,2304]{1,0:T(8,128)(2,1)}, bf16[48,768]{1,0:T(8,128)(2,1)}, bf16[48,3072]{1,0:T(8,128)(2,1)}, bf16[192,768]{1,0:T(8,128)(2,1)}) async-done(((bf16[48,2304]{1,0:T(8,128)(2,1)}, bf16[48,768]{1,0:T(8,128)(2,1)}, bf16[48,3072]{1,0:T(8,128)(2,1)}, bf16[192,768]{1,0:T(8,128)(2,1)}), (bf16[48,2304]{1,0:T(8,128)(2,1)}, bf16[48,768]{1,0:T(8,128)(2,1)}, ...) | async-done | bytes 884752 | tf_op jit(solution)/shard_map/psum | solution.py:242
  (288 shorter events, 306.3 us)
Async XLA Ops:
  7.2 79.5 %copy-start.2 = (bf16[5,416,768]{2,1,0:T(8,128)(2,1)S(1)}, bf16[5,416,768]{2,1,0:T(8,128)(2,1)}, u32[]{:S(2)}) copy-start(bf16[5,416,768]{2,1,0:T(8,128)(2,1)} %param.19) | copy-start | bytes 9584644
  7.2 11.0 %copy-start.42 = (bf16[48]{0:T(256)(128)(2,1)S(1)}, bf16[48]{0:T(256)(128)(2,1)}, u32[]{:S(2)}) copy-start(bf16[48]{0:T(256)(128)(2,1)} %param.21) | copy-start | bytes 292
  7.2 11.2 %copy-start.43 = (bf16[48]{0:T(256)(128)(2,1)S(1)}, bf16[48]{0:T(256)(128)(2,1)}, u32[]{:S(2)}) copy-start(bf16[48]{0:T(256)(128)(2,1)} %param.22) | copy-start | bytes 292
  7.2 11.5 %copy-start.44 = (bf16[48]{0:T(256)(128)(2,1)S(1)}, bf16[48]{0:T(256)(128)(2,1)}, u32[]{:S(2)}) copy-start(bf16[48]{0:T(256)(128)(2,1)} %param.26) | copy-start | bytes 292
  7.2 11.7 %copy-start.45 = (bf16[48]{0:T(256)(128)(2,1)S(1)}, bf16[48]{0:T(256)(128)(2,1)}, u32[]{:S(2)}) copy-start(bf16[48]{0:T(256)(128)(2,1)} %param.27) | copy-start | bytes 292
  7.2 11.9 %copy-start.46 = (bf16[48]{0:T(256)(128)(2,1)S(1)}, bf16[48]{0:T(256)(128)(2,1)}, u32[]{:S(2)}) copy-start(bf16[48]{0:T(256)(128)(2,1)} %param.28) | copy-start | bytes 292
  7.3 12.1 %copy-start.47 = (bf16[48]{0:T(256)(128)(2,1)S(1)}, bf16[48]{0:T(256)(128)(2,1)}, u32[]{:S(2)}) copy-start(bf16[48]{0:T(256)(128)(2,1)} %param.32) | copy-start | bytes 292
  7.3 12.4 %copy-start.48 = (bf16[192]{0:T(256)(128)(2,1)S(1)}, bf16[192]{0:T(256)(128)(2,1)}, u32[]{:S(2)}) copy-start(bf16[192]{0:T(256)(128)(2,1)} %param.30) | copy-start | bytes 1156
  7.3 12.6 %copy-start.49 = (bf16[96]{0:T(256)(128)(2,1)S(1)}, bf16[96]{0:T(256)(128)(2,1)}, u32[]{:S(2)}) copy-start(bf16[96]{0:T(256)(128)(2,1)} %param.24) | copy-start | bytes 580
  7.3 84.4 %all-gather.5.cloned.1.call-start = ((), (), s32[]{:S(2)}) async-start(), calls=%async_computation.4 | async-start | bytes 3760128 | tf_op jit(solution)/shard_map/all_gather | solution.py:85
  8.0 237.3 %all-gather.7.cloned.1.call-start = ((), (), s32[]{:S(2)}) async-start(), calls=%async_computation.5 | async-start | bytes 1253376 | tf_op jit(solution)/shard_map/all_gather | solution.py:87
  8.8 251.8 %all-gather.9.cloned.1.call-start = ((), (), s32[]{:S(2)}) async-start(), calls=%async_computation.6 | async-start | bytes 5013504 | tf_op jit(solution)/shard_map/all_gather | solution.py:113
  9.5 322.6 %all-gather.11.cloned.1.call-start = ((), (), s32[]{:S(2)}) async-start(), calls=%async_computation.7 | async-start | bytes 5013504 | tf_op jit(solution)/shard_map/all_gather | solution.py:115
  10.1 774.1 %reduce-scatter.7.cloned.1.call-start = ((), (), s32[]{:S(2)}) async-start(), calls=%async_computation.9 | async-start | bytes 2506752 | tf_op jit(solution)/shard_map/reduce_scatter | solution.py:236
  15.6 76.1 %copy-start.14 = (f32[2080]{0:T(1024)}, f32[2080]{0:T(1024)S(1)}, u32[]{:S(2)}) copy-start(f32[2080]{0:T(1024)S(1)} %div.47) | copy-start | bytes 24964
  136.1 10.8 %copy-start.10 = (bf16[2080,768]{1,0:T(8,128)(2,1)S(1)}, bf16[2080,768]{1,0:T(8,128)(2,1)}, u32[]{:S(2)}) copy-start(bf16[2080,768]{1,0:T(8,128)(2,1)} %slice.33) | copy-start | bytes 9584644
  256.3 126.3 %copy-start.20 = (f32[2080]{0:T(1024)}, f32[2080]{0:T(1024)S(1)}, u32[]{:S(2)}) copy-start(f32[2080]{0:T(1024)S(1)} %broadcast_multiply_fusion.1) | copy-start | bytes 24964
  260.6 122.0 %copy-start.26 = (f32[2080]{0:T(1024)}, f32[2080]{0:T(1024)S(1)}, u32[]{:S(2)}) copy-start(f32[2080]{0:T(1024)S(1)} %fusion.69) | copy-start | bytes 24964
  260.6 71.5 %copy-start.5 = (bf16[5,416,768]{2,1,0:T(8,128)(2,1)S(1)}, bf16[5,416,768]{2,1,0:T(8,128)(2,1)}, u32[]{:S(2)}) copy-start(bf16[5,416,768]{2,1,0:T(8,128)(2,1)} %param.33) | copy-start | bytes 9584644
  360.5 22.1 %copy-start.23 = (f32[2080]{0:T(1024)S(1)}, f32[2080]{0:T(1024)}, u32[]{:S(2)}) copy-start(f32[2080]{0:T(1024)} %copy-done.22) | copy-start | bytes 24964
  360.5 22.1 %copy-start.1 = (f32[2080,768]{1,0:T(8,128)S(1)}, f32[2080,768]{1,0:T(8,128)}, u32[]{:S(2)}) copy-start(f32[2080,768]{1,0:T(8,128)} %fusion.67) | copy-start | bytes 19169284
  424.2 361.5 %reduce-scatter.5.cloned.1.call-start = ((), (), s32[]{:S(2)}) async-start(), calls=%async_computation.8 | async-start | bytes 7520256 | tf_op jit(solution)/shard_map/reduce_scatter | solution.py:234
  621.6 202.2 %reduce-scatter.9.cloned.1.call-start = ((), (), s32[]{:S(2)}) async-start(), calls=%async_computation.10 | async-start | bytes 10027008 | tf_op jit(solution)/shard_map/reduce_scatter | solution.py:170
  641.7 297.1 %reduce-scatter.11.cloned.1.call-start = ((), (), s32[]{:S(2)}) async-start(), calls=%async_computation.11 | async-start | bytes 10027008 | tf_op jit(solution)/shard_map/reduce_scatter | solution.py:172
  659.4 319.4 %all-reduce.22.cloned.1.call-start = ((), (), s32[]{:S(2)}) async-start(), calls=%async_computation.12 | async-start | bytes 1769472 | tf_op jit(solution)/shard_map/psum | solution.py:242
  668.9 19.6 %copy-start.32 = (f32[768]{0:T(1024)S(1)}, f32[768]{0:T(1024)}, u32[]{:S(2)}) copy-start(f32[768]{0:T(1024)} %get-tuple-element.230) | copy-start | bytes 9220
  668.9 19.6 %copy-start.34 = (f32[3072]{0:T(1024)S(1)}, f32[3072]{0:T(1024)}, u32[]{:S(2)}) copy-start(f32[3072]{0:T(1024)} %get-tuple-element.251) | copy-start | bytes 36868
  668.9 19.6 %copy-start.38 = (f32[768]{0:T(1024)S(1)}, f32[768]{0:T(1024)}, u32[]{:S(2)}) copy-start(f32[768]{0:T(1024)} %get-tuple-element.162) | copy-start | bytes 9220
  668.9 19.6 %copy-start.39 = (f32[768]{0:T(1024)S(1)}, f32[768]{0:T(1024)}, u32[]{:S(2)}) copy-start(f32[768]{0:T(1024)} %get-tuple-element.164) | copy-start | bytes 9220
  668.9 87.8 %copy-start.25 = (f32[2080]{0:T(1024)S(1)}, f32[2080]{0:T(1024)}, u32[]{:S(2)}) copy-start(f32[2080]{0:T(1024)} %copy-done.24) | copy-start | bytes 24964
  767.2 173.5 %copy-start.7 = (bf16[5,416,768]{2,1,0:T(8,128)(2,1)S(1)}, bf16[5,416,768]{2,1,0:T(8,128)(2,1)}, u32[]{:S(2)}) copy-start(bf16[5,416,768]{2,1,0:T(8,128)(2,1)} %param.33) | copy-start | bytes 9584644
  767.2 173.5 %copy-start.19 = (f32[2080]{0:T(1024)S(1)}, f32[2080]{0:T(1024)}, u32[]{:S(2)}) copy-start(f32[2080]{0:T(1024)} %copy-done.18) | copy-start | bytes 24964
  (27 other events, 149.3 us)
Sparse Core Ops, SparseCore 0:
  10.4 50.3 all-gather.4
  63.1 36.6 all-gather.6
  102.1 51.9 all-gather.8
  156.3 51.6 all-gather.10
  424.3 60.4 reduce-scatter.6
  621.7 87.2 reduce-scatter.4
  713.1 110.7 reduce-scatter.8
  827.9 110.8 reduce-scatter.10
  942.5 36.2 all-reduce.21
where the time goes:
time: 1000 us; the launch traced here: 992 us
  matrix products  370 us (37%)
  local copies, waits for them, and re-layouts  185 us (18%)
  waiting for transfers between devices  183 us (18%)
  blocking collectives  127 us (13%)
  other arithmetic  107 us (11%)
  between operations  18.9 us (2%)
    unnamed x2, blocking collectives  122 us
    reduce_scatter x1, waiting for transfers between devices, per_device(): lax.psum_scatter(mlp_local[4], 'fsdp', scatter_dimension=0, tiled=True)  113 us
    dot_general x1, matrix products, per_device(): jnp.dot(normed_two_low, up_full, preferred_element_type=jnp.float32)  71.5 us
    while x4, local copies, waits for them, and re-layouts, per_device(): lax.map(row_forward, (queries, keys_all, values_all, segment_ids))  39.8 us
    reduce_scatter x1, waiting for transfers between devices, per_device(): lax.psum_scatter(mlp_local[2], 'fsdp', scatter_dimension=0, tiled=True)  36.4 us
    while x4, local copies, waits for them, and re-layouts, per_device(): lax.map(row_backward, (queries, keys_all, values_all, segment_ids, grad_m...  33.9 us
    psum x1, waiting for transfers between devices, per_device(): lax.psum(attn_owned[2].astype(jnp.bfloat16), 'dp').astype(jnp.float32)  31.1 us
    dot_general x10, matrix products, masked_scores(): jnp.einsum('qhe,khe->hqk', queries, keys_row, preferred_element_type=jnp....  31.1 us
  transfers between devices with their start and end apart: 9, of which 3 were waited for; matrix products, arithmetic and copies ran while one was open for 56% of the time, Pallas kernels for 0%

commit v1 on v0

--- a/solution.py
+++ b/solution.py
@@ -4,6 +4,11 @@
 from jax.sharding import PartitionSpec as P
 
 HEAD_DIM = 64
+
+
+def summed_here(x, mesh_axis):
+    terms = lax.all_gather(x, mesh_axis)
+    return jnp.sum(terms, axis=0)
 
 
 def layer_norm(values, gain, shift):
@@ -239,7 +244,7 @@
     attn_summed = (
         lax.psum(attn_owned[0].astype(jnp.bfloat16), "dp").astype(jnp.float32),
         lax.psum(attn_owned[1].astype(jnp.bfloat16), "dp").astype(jnp.float32),
-        lax.psum(attn_owned[2].astype(jnp.bfloat16), "dp").astype(jnp.float32),
+        summed_here(attn_owned[2].astype(jnp.bfloat16), "dp").astype(jnp.float32),
         lax.psum(attn_owned[3].astype(jnp.bfloat16), "dp").astype(jnp.float32),
         lax.psum(attn_owned[4].astype(jnp.bfloat16), "dp").astype(jnp.float32),
         lax.psum(attn_owned[5].astype(jnp.bfloat16), "dp").astype(jnp.float32),

time: 1000 us -> 841 us (0.84)
  waiting for transfers between devices: 183 us -> 19.2 us
  blocking collectives: 127 us -> 139 us
    reduce_scatter x1, waiting for transfers between devices: 113 us -> 0.01 us  [per_device(): lax.psum_scatter(mlp_local[4], 'fsdp', scatter_dimension=0, tiled=True)]
    reduce_scatter x1, waiting for transfers between devices: 36.4 us -> 0.01 us  [per_device(): lax.psum_scatter(mlp_local[2], 'fsdp', scatter_dimension=0, tiled=True)]
    psum x1, waiting for transfers between devices: 31.1 us -> 16.4 us  [per_device(): lax.psum(attn_owned[4].astype(jnp.bfloat16), 'dp').astype(jnp.float32)]
  transfers between devices with their start and end apart: 9 -> 9, of which waited for: 3 -> 1; matrix products, arithmetic and copies ran while one was open for 56% -> 69% of each run, Pallas kernels for 0% -> 0%
where the time goes in v1:
time: 841 us; the launch traced here: 833 us
  matrix products  367 us (44%)
  local copies, waits for them, and re-layouts  183 us (22%)
  blocking collectives  139 us (17%)
  other arithmetic  104 us (12%)
  waiting for transfers between devices  19.2 us (2%)
  between operations  18.9 us (2%)
    unnamed x2, blocking collectives  124 us
    dot_general x1, matrix products, per_device(): jnp.dot(normed_two_low, up_full, preferred_element_type=jnp.float32)  71.4 us
    while x4, local copies, waits for them, and re-layouts, per_device(): lax.map(row_forward, (queries, keys_all, values_all, segment_ids))  39.8 us
    while x4, local copies, waits for them, and re-layouts, per_device(): lax.map(row_backward, (queries, keys_all, values_all, segment_ids, grad_m...  34.5 us
    dot_general x10, matrix products, masked_scores(): jnp.einsum('qhe,khe->hqk', queries, keys_row, preferred_element_type=jnp....  31.1 us
    dot_general x1, matrix products, per_device(): jnp.einsum('nd,fd->nf', cotangent, down_back, preferred_element_type=jnp....  28.4 us
    dot_general x5, matrix products, row_backward(): jnp.einsum('qhe,khe->hqk', grad_mixed, values_row, preferred_element_type...  24.9 us
    dot_general x5, matrix products, row_forward(): jnp.einsum('hqk,khe->qhe', probs, values_row, preferred_element_type=jnp....  24.8 us
  transfers between devices with their start and end apart: 9, of which 1 were waited for; matrix products, arithmetic and copies ran while one was open for 69% of the time, Pallas kernels for 0%

profile of v1, /device:TPU:0, one launch (start us, length us, event | category | flops | bytes accessed | tf_op | source)
XLA Modules:
  0.0 832.6 jit_solution(475523369117711037)
XLA Ops:
  20.1 64.0 %all-reduce.17 = (bf16[768]{0:T(1024)(128)(2,1)S(1)}, bf16[768]{0:T(1024)(128)(2,1)S(1)}, bf16[1536]{0:T(1024)(128)(2,1)S(1)}, bf16[768]{0:T(1024)(128)(2,1)S(1)...) all-reduce(bf16[768]{0:T(1024)(128)(2,1)S(1)} %dynamic-update-slice, ...), channel_id=1, replica_groups=mesh['fsdp'=16,'dp'=2] {'fsdp'}, use_global_device_ids=true, to_apply=%add.1 | all-reduce | flops 9216 | bytes 36864
  91.7 10.9 %fusion.78 = f32[2080,2304]{1,0:T(8,128)S(1)} fusion(bf16[2080,768]{1,0:T(8,128)(2,1)} %get-tuple-element.242, bf16[768,2304]{1,0:T(8,128)(2,1)} %all-gather.6.cloned.1.call-done), kind=kOutput, calls=%fused_computation.139 | convolution fusion | flops 7361003520 | bytes 25903104 | tf_op jit(solution)/shard_map/dot_general | solution.py:101
  106.9 10.8 %reshape.304 = bf16[5,416,12,64]{3,2,1,0:T(8,128)(2,1)} reshape(bf16[2080,768]{1,0:T(8,128)(2,1)} %get-tuple-element.240) | data formatting | bytes 6389760 | tf_op jit(solution)/shard_map/reshape | solution.py:106
  117.8 10.6 %copy.66 = bf16[5,416,12,64]{1,3,2,0:T(8,128)(2,1)} copy(bf16[5,416,12,64]{3,2,1,0:T(8,128)(2,1)} %reshape.304) | data formatting | bytes 6389760 | tf_op jit(solution)/shard_map/while | solution.py:108
  128.4 7.7 reshape.305
  136.1 10.8 %copy.67 = bf16[5,416,12,64]{1,3,2,0:T(8,128)(2,1)} copy(bf16[5,416,12,64]{3,2,1,0:T(8,128)(2,1)} %reshape.305) | data formatting | bytes 6389760 | tf_op jit(solution)/shard_map/while | solution.py:108
  146.9 8.2 reshape.306
  155.0 10.7 %copy.68 = bf16[5,416,12,64]{1,3,2,0:T(8,128)(2,1)} copy(bf16[5,416,12,64]{3,2,1,0:T(8,128)(2,1)} %reshape.306) | data formatting | bytes 6389760 | tf_op jit(solution)/shard_map/while | solution.py:108
  168.1 59.9 %while.26 = (s32[]{:T(128)}, bf16[5,416,12,64]{1,3,2,0:T(8,128)(2,1)}, f32[5,12,416]{2,1,0:T(8,128)}, bf16[5,416,12,64]{1,3,2,0:T(8,128)(2,1)}, s32[5,416]{1,0:T...) while((s32[]{:T(128)}, bf16[5,416,12,64]{1,3,2,0:T(8,128)(2,1)}, ...), condition=%wide.region_5.6_spmd, body=%wide.region_2.5_spmd.sunk | while | flops 557035648 | bytes 28938200 | solution.py:108
  228.0 7.7 copy.69
  235.8 9.6 %reshape.245 = bf16[2080,768]{0,1:T(8,128)(2,1)} reshape(bf16[5,416,12,64]{1,0,3,2:T(8,128)(2,1)} %copy.69) | data formatting | bytes 6389760 | tf_op jit(solution)/shard_map/reshape | solution.py:109
  245.4 7.7 fusion.67
  260.6 71.4 %multiply_convert_fusion.3 = (bf16[2080,3072]{1,0:T(8,128)(2,1)}, f32[2080,3072]{1,0:T(8,128)}, f32[2080,3072]{1,0:T(8,128)}) fusion(f32[3072]{0:T(1024)S(1)} %copy-done.27, bf16[768,3072]{1,0:T(8,128)(2,1)} %all-gather.10.cloned.1.call-done, f32[2080,768]{1,0:T(8,128)} %fusion.67, f32[768]{0:T(1024)S(1)} %copy-done.29, f32[768]{0:T(1024)S(1)} %copy-done.25, ...), kind=kOutput, calls=%fused_computation.68 | convolution fusion | flops 10244382720 | bytes 75041024 | tf_op jit(solution)/shard_map/dot_general | solution.py:128
  332.1 28.4 %convert_reduce_fusion = (f32[3072]{0:T(1024)}, bf16[2080,3072]{1,0:T(8,128)(2,1)}) fusion(f32[2080,3072]{1,0:T(8,128)} %get-tuple-element.234, bf16[2080,768]{1,0:T(8,128)(2,1)S(1)} %bitcast.162, bf16[3072,768]{1,0:T(8,128)(2,1)} %all-gather.12.cloned.1.call-done, f32[2080,3072]{1,0:T(8,128)} %get-tuple-element.247, f32[3072]{0:T(1024)S(1)} %copy-done.27), kind=kOutput, calls=%fused_computation.66 | convolution fusion | flops 9923294208 | bytes 71835648 | tf_op jit(solution)/shard_map/nd,fd->nf/dot_general | solution.py:155
  360.5 22.0 %multiply_reduce_fusion.1 = (f32[768]{0:T(1024)}, f32[2080]{0:T(1024)S(1)}, f32[768]{0:T(1024)}, f32[2080,768]{1,0:T(8,128)}) fusion(f32[2080,768]{1,0:T(8,128)} %fusion.67, f32[2080]{0:T(1024)S(1)} %fusion.69, f32[2080]{0:T(1024)S(1)} %broadcast_multiply_fusion.1, f32[768]{0:T(1024)S(1)} %copy-done.25, bf16[2080,3072]{1,0:T(8,128)(2,1)} %get-tuple-element.251, ...), kind=kOutput, calls=%fused_computation.98 | convolution fusion | flops 9827446784 | bytes 30311808 | tf_op jit(solution)/shard_map/nf,df->nd/dot_general | solution.py:161
  397.6 19.0 %fusion.70 = f32[768,3072]{1,0:T(8,128)} fusion(bf16[2080,3072]{1,0:T(8,128)(2,1)} %get-tuple-element.251, f32[2080,768]{1,0:T(8,128)} %fusion.67, f32[768]{0:T(1024)S(1)} %copy-done.29, f32[768]{0:T(1024)S(1)} %copy-done.25, f32[2080]{0:T(1024)S(1)} %fusion.69, f32[2080]{0:T(1024)S(1)} %broadcast_multiply_fusion.1), kind=kOutput, calls=%fused_computation.133 | convolution fusion | flops 9822658560 | bytes 28629248 | tf_op jit(solution)/shard_map/nd,nf->df/dot_general | solution.py:158
  422.0 10.8 %reshape.295 = bf16[5,416,12,64]{3,2,1,0:T(8,128)(2,1)} reshape(bf16[2080,768]{1,0:T(8,128)(2,1)} %convolution_convert_fusion) | data formatting | bytes 6389760 | tf_op jit(solution)/shard_map/reshape | solution.py:208
  432.8 10.8 %copy.73 = bf16[5,416,12,64]{1,3,2,0:T(8,128)(2,1)} copy(bf16[5,416,12,64]{3,2,1,0:T(8,128)(2,1)} %reshape.295) | data formatting | bytes 6389760 | tf_op jit(solution)/shard_map/while | solution.py:206
  443.6 15.9 %fusion.81 = f32[3072,768]{1,0:T(8,128)} fusion(bf16[2080,3072]{1,0:T(8,128)(2,1)} %get-tuple-element.233, bf16[2080,768]{1,0:T(8,128)(2,1)S(1)} %bitcast.163), kind=kOutput, calls=%fused_computation.142 | convolution fusion | flops 9814671360 | bytes 25411584 | tf_op jit(solution)/shard_map/nf,nd->fd/dot_general | solution.py:152
  466.6 121.9 %while.27 = (s32[]{:T(128)}, bf16[5,416,12,64]{1,3,2,0:T(8,128)(2,1)}, bf16[5,416,12,64]{1,3,2,0:T(8,128)(2,1)}, bf16[5,416,12,64]{1,3,2,0:T(8,128)(2,1)}, bf16[...) while((s32[]{:T(128)}, ...), condition=%wide.region_12.13_spmd, body=%wide.region_10.12_spmd.sunk | while | flops 1361985664 | bytes 71006704 | solution.py:206
  588.5 8.4 %copy.75 = bf16[5,416,12,64]{1,0,3,2:T(8,128)(2,1)} copy(bf16[5,416,12,64]{1,3,2,0:T(8,128)(2,1)} %get-tuple-element.108) | data formatting | bytes 6389760 | tf_op jit(solution)/shard_map/while | solution.py:206
  596.9 8.4 %reshape.249 = bf16[2080,768]{0,1:T(8,128)(2,1)S(1)} reshape(bf16[5,416,12,64]{1,0,3,2:T(8,128)(2,1)} %copy.75) | data formatting | bytes 6389760 | tf_op jit(solution)/shard_map/reshape | solution.py:210
  613.0 9.5 %reshape.250 = bf16[2080,768]{0,1:T(8,128)(2,1)} reshape(bf16[5,416,12,64]{1,0,3,2:T(8,128)(2,1)} %copy.76) | data formatting | bytes 6389760 | tf_op jit(solution)/shard_map/reshape | solution.py:211
  622.5 7.7 copy.77
  630.2 9.5 %reshape.251 = bf16[2080,768]{0,1:T(8,128)(2,1)} reshape(bf16[5,416,12,64]{1,0,3,2:T(8,128)(2,1)} %copy.77) | data formatting | bytes 6389760 | tf_op jit(solution)/shard_map/reshape | solution.py:212
  647.1 10.6 %fusion.79 = f32[768,2304]{1,0:T(8,128)} fusion(bf16[2080,768]{1,0:T(8,128)(2,1)S(1)} %copy-done.11, bf16[2080,2304]{0,1:T(8,128)(2,1)S(1)} %constant_dynamic-update-slice_fusion), kind=kOutput, calls=%fused_computation.140 | convolution fusion | flops 7361003520 | bytes 19857408 | tf_op jit(solution)/shard_map/nd,nc->dc/dot_general | solution.py:220
  662.6 17.1 %fusion.72 = (f32[768]{0:T(1024)S(1)}, f32[2080]{0:T(1024)S(1)}, f32[768]{0:T(1024)S(1)}, f32[2080,768]{1,0:T(8,128)S(1)}) fusion(f32[2080,768]{1,0:T(8,128)} %get-tuple-element.241, f32[768]{0:T(1024)S(1)} %copy-done.24, f32[2080]{0:T(1024)S(1)} %copy-done.16, f32[2080]{0:T(1024)S(1)} %copy-done.14, bf16[5,416,768]{2,1,0:T(8,128)(2,1)S(1)} %copy-done.4, ...), kind=kOutput, calls=%fused_computation.135 | convolution fusion | flops 7375376384 | bytes 29132160 | tf_op jit(solution)/shard_map/nc,dc->nd/dot_general | solution.py:223
  687.7 8.2 add_convert_fusion.1
  695.9 16.4 %add_convert_fusion.2 = bf16[2080,768]{1,0:T(8,128)(2,1)} fusion(f32[2080,768]{1,0:T(8,128)S(1)} %bitcast.161, bf16[2080,3072]{1,0:T(8,128)(2,1)} %get-tuple-element.233, bf16[3072,768]{1,0:T(8,128)(2,1)} %all-gather.12.cloned.1.call-done, f32[768]{0:T(1024)S(1)} %convert_element_type.207), kind=kOutput, calls=%fused_computation.105 | convolution fusion | flops 9819463680 | bytes 27085824 | tf_op jit(solution)/shard_map/dot_general | solution.py:135
  722.3 60.4 %all-reduce.16 = (bf16[768]{0:T(1024)(128)(2,1)S(1)}, bf16[768]{0:T(1024)(128)(2,1)S(1)}, bf16[1536]{0:T(1024)(128)(2,1)S(1)}, bf16[768]{0:T(1024)(128)(2,1)S(1)...) all-reduce(f32[768]{0:T(1024)S(1)} %get-tuple-element.167, ...), channel_id=3, replica_groups=mesh['fsdp'=16,'dp'=2] {'fsdp'}, use_global_device_ids=true, to_apply=%region_16.17.clone | all-reduce | flops 9216 | bytes 55296
  793.4 9.7 %all-gather = bf16[96,2304]{1,0:T(8,128)(2,1)S(1)} all-gather(bf16[48,2304]{1,0:T(8,128)(2,1)S(1)} %convert_element_type.218), channel_id=2, replica_groups=mesh['fsdp'=16,'dp'=2] {'dp'}, dimensions={0}, use_global_device_ids=true | all-gather | bytes 663552 | tf_op jit(solution)/shard_map/all_gather | solution.py:10
  804.1 16.4 %all-reduce.22.cloned.1.call-done = (bf16[48,768]{1,0:T(8,128)(2,1)}, bf16[48,3072]{1,0:T(8,128)(2,1)}, bf16[192,768]{1,0:T(8,128)(2,1)}) async-done(((bf16[48,768]{1,0:T(8,128)(2,1)}, bf16[48,3072]{1,0:T(8,128)(2,1)}, bf16[192,768]{1,0:T(8,128)(2,1)}), (bf16[48,768]{1,0:T(8,128)(2,1)}, bf16[48,3072]{1,0:T(8,128)(2,1)}, bf16[192,768]{1,0:T(8,128)(2,1)})) %all-reduce.22.cloned.1.call-update) | async-done | bytes 663568 | tf_op jit(solution)/shard_map/psum | solution.py:249
  (281 shorter events, 293.7 us)
Async XLA Ops:
  7.2 79.5 %copy-start.2 = (bf16[5,416,768]{2,1,0:T(8,128)(2,1)S(1)}, bf16[5,416,768]{2,1,0:T(8,128)(2,1)}, u32[]{:S(2)}) copy-start(bf16[5,416,768]{2,1,0:T(8,128)(2,1)} %param.19) | copy-start | bytes 9584644
  7.2 11.0 %copy-start.35 = (bf16[48]{0:T(256)(128)(2,1)S(1)}, bf16[48]{0:T(256)(128)(2,1)}, u32[]{:S(2)}) copy-start(bf16[48]{0:T(256)(128)(2,1)} %param.21) | copy-start | bytes 292
  7.2 11.2 %copy-start.36 = (bf16[48]{0:T(256)(128)(2,1)S(1)}, bf16[48]{0:T(256)(128)(2,1)}, u32[]{:S(2)}) copy-start(bf16[48]{0:T(256)(128)(2,1)} %param.22) | copy-start | bytes 292
  7.2 11.5 %copy-start.37 = (bf16[48]{0:T(256)(128)(2,1)S(1)}, bf16[48]{0:T(256)(128)(2,1)}, u32[]{:S(2)}) copy-start(bf16[48]{0:T(256)(128)(2,1)} %param.26) | copy-start | bytes 292
  7.2 11.7 %copy-start.38 = (bf16[48]{0:T(256)(128)(2,1)S(1)}, bf16[48]{0:T(256)(128)(2,1)}, u32[]{:S(2)}) copy-start(bf16[48]{0:T(256)(128)(2,1)} %param.27) | copy-start | bytes 292
  7.2 11.9 %copy-start.39 = (bf16[48]{0:T(256)(128)(2,1)S(1)}, bf16[48]{0:T(256)(128)(2,1)}, u32[]{:S(2)}) copy-start(bf16[48]{0:T(256)(128)(2,1)} %param.28) | copy-start | bytes 292
  7.3 12.1 %copy-start.40 = (bf16[48]{0:T(256)(128)(2,1)S(1)}, bf16[48]{0:T(256)(128)(2,1)}, u32[]{:S(2)}) copy-start(bf16[48]{0:T(256)(128)(2,1)} %param.32) | copy-start | bytes 292
  7.3 12.4 %copy-start.41 = (bf16[192]{0:T(256)(128)(2,1)S(1)}, bf16[192]{0:T(256)(128)(2,1)}, u32[]{:S(2)}) copy-start(bf16[192]{0:T(256)(128)(2,1)} %param.30) | copy-start | bytes 1156
  7.3 12.6 %copy-start.42 = (bf16[96]{0:T(256)(128)(2,1)S(1)}, bf16[96]{0:T(256)(128)(2,1)}, u32[]{:S(2)}) copy-start(bf16[96]{0:T(256)(128)(2,1)} %param.24) | copy-start | bytes 580
  7.3 84.4 %all-gather.6.cloned.1.call-start = ((), (), s32[]{:S(2)}) async-start(), calls=%async_computation.4 | async-start | bytes 3760128 | tf_op jit(solution)/shard_map/all_gather | solution.py:90
  8.0 237.4 %all-gather.8.cloned.1.call-start = ((), (), s32[]{:S(2)}) async-start(), calls=%async_computation.5 | async-start | bytes 1253376 | tf_op jit(solution)/shard_map/all_gather | solution.py:92
  8.8 251.8 %all-gather.10.cloned.1.call-start = ((), (), s32[]{:S(2)}) async-start(), calls=%async_computation.6 | async-start | bytes 5013504 | tf_op jit(solution)/shard_map/all_gather | solution.py:118
  9.5 322.6 %all-gather.12.cloned.1.call-start = ((), (), s32[]{:S(2)}) async-start(), calls=%async_computation.7 | async-start | bytes 5013504 | tf_op jit(solution)/shard_map/all_gather | solution.py:120
  10.1 702.3 %reduce-scatter.7.cloned.1.call-start = ((), (), s32[]{:S(2)}) async-start(), calls=%async_computation.9 | async-start | bytes 2506752 | tf_op jit(solution)/shard_map/reduce_scatter | solution.py:241
  15.6 76.1 %copy-start.13 = (f32[2080]{0:T(1024)}, f32[2080]{0:T(1024)S(1)}, u32[]{:S(2)}) copy-start(f32[2080]{0:T(1024)S(1)} %div.47) | copy-start | bytes 24964
  136.1 10.8 %copy-start.9 = (bf16[2080,768]{1,0:T(8,128)(2,1)S(1)}, bf16[2080,768]{1,0:T(8,128)(2,1)}, u32[]{:S(2)}) copy-start(bf16[2080,768]{1,0:T(8,128)(2,1)} %slice.33) | copy-start | bytes 9584644
  235.8 9.7 %copy-start.3 = (bf16[5,416,768]{2,1,0:T(8,128)(2,1)S(1)}, bf16[5,416,768]{2,1,0:T(8,128)(2,1)}, u32[]{:S(2)}) copy-start(bf16[5,416,768]{2,1,0:T(8,128)(2,1)} %param.19) | copy-start | bytes 9584644
  235.8 9.7 %copy-start.30 = (f32[768]{0:T(1024)S(1)}, f32[768]{0:T(1024)}, u32[]{:S(2)}) copy-start(f32[768]{0:T(1024)} %convert_element_type.201) | copy-start | bytes 9220
  260.6 71.5 %copy-start.5 = (bf16[5,416,768]{2,1,0:T(8,128)(2,1)S(1)}, bf16[5,416,768]{2,1,0:T(8,128)(2,1)}, u32[]{:S(2)}) copy-start(bf16[5,416,768]{2,1,0:T(8,128)(2,1)} %param.33) | copy-start | bytes 9584644
  360.5 22.0 %copy-start.20 = (f32[2080]{0:T(1024)S(1)}, f32[2080]{0:T(1024)}, u32[]{:S(2)}) copy-start(f32[2080]{0:T(1024)} %copy-done.19) | copy-start | bytes 24964
  360.5 22.0 %copy-start.1 = (f32[2080,768]{1,0:T(8,128)S(1)}, f32[2080,768]{1,0:T(8,128)}, u32[]{:S(2)}) copy-start(f32[2080,768]{1,0:T(8,128)} %fusion.67) | copy-start | bytes 19169284
  397.5 316.4 %reduce-scatter.9.cloned.1.call-start = ((), (), s32[]{:S(2)}) async-start(), calls=%async_computation.10 | async-start | bytes 10027008 | tf_op jit(solution)/shard_map/reduce_scatter | solution.py:175
  416.6 299.1 %reduce-scatter.11.cloned.1.call-start = ((), (), s32[]{:S(2)}) async-start(), calls=%async_computation.11 | async-start | bytes 10027008 | tf_op jit(solution)/shard_map/reduce_scatter | solution.py:177
  432.8 10.8 %copy-start.6 = (bf16[5,416,768]{2,1,0:T(8,128)(2,1)S(1)}, bf16[5,416,768]{2,1,0:T(8,128)(2,1)}, u32[]{:S(2)}) copy-start(bf16[5,416,768]{2,1,0:T(8,128)(2,1)} %param.33) | copy-start | bytes 9584644
  459.5 332.9 %reduce-scatter.5.cloned.1.call-start = ((), (), s32[]{:S(2)}) async-start(), calls=%async_computation.8 | async-start | bytes 7520256 | tf_op jit(solution)/shard_map/reduce_scatter | solution.py:239
  657.7 162.8 %all-reduce.22.cloned.1.call-start = ((), (), s32[]{:S(2)}) async-start(), calls=%async_computation.12 | async-start | bytes 1327104 | tf_op jit(solution)/shard_map/psum | solution.py:249
  662.6 17.1 %copy-start.22 = (f32[2080]{0:T(1024)S(1)}, f32[2080]{0:T(1024)}, u32[]{:S(2)}) copy-start(f32[2080]{0:T(1024)} %copy-done.21) | copy-start | bytes 24964
  684.3 11.6 %slice-start = ((s8[6389760]{0:T(1024)(128)(4,1)}), s8[2195456]{0:T(1024)(128)(4,1)S(1)}, s32[]{:S(2)}) async-start(s8[6389760]{0:T(1024)(128)(4,1)} %bitcast.160), calls=%async_computation.13 | async-start | bytes 4390912
  712.3 9.9 %copy-start.26 = (f32[768]{0:T(1024)S(1)}, f32[768]{0:T(1024)}, u32[]{:S(2)}) copy-start(f32[768]{0:T(1024)} %get-tuple-element.229) | copy-start | bytes 9220
  712.3 9.9 %copy-start.28 = (f32[3072]{0:T(1024)S(1)}, f32[3072]{0:T(1024)}, u32[]{:S(2)}) copy-start(f32[3072]{0:T(1024)} %get-tuple-element.250) | copy-start | bytes 36868
  712.3 10.0 %copy-start.31 = (f32[768]{0:T(1024)S(1)}, f32[768]{0:T(1024)}, u32[]{:S(2)}) copy-start(f32[768]{0:T(1024)} %get-tuple-element.162) | copy-start | bytes 9220
  712.3 10.0 %copy-start.32 = (f32[768]{0:T(1024)S(1)}, f32[768]{0:T(1024)}, u32[]{:S(2)}) copy-start(f32[768]{0:T(1024)} %get-tuple-element.164) | copy-start | bytes 9220
  (22 other events, 119.3 us)
Sparse Core Ops, SparseCore 0:
  10.4 50.2 all-gather.5
  63.0 36.8 all-gather.7
  102.1 51.9 all-gather.9
  156.3 51.6 all-gather.11
  397.6 60.5 reduce-scatter.6
  462.2 110.2 reduce-scatter.8
  576.6 110.8 reduce-scatter.10
  691.5 90.4 reduce-scatter.4
  785.6 34.8 all-reduce.21
